TPU v7x, 32 devices: a whole 2x2x4 slice. The times are simulated.
32 devices in a mesh: row: 8 (over z, core), col: 4 (over y, x).
Axes of the slice: x: 2, y: 2, z: 4, core: 2. Of those that a mesh axis runs over, the one named last changes fastest.
Arguments:
- patches: bfloat16 [3, 128, 128, 1024], P(None, 'row', 'col'), may hold values from -6 to 6
- registers: bfloat16 [3, 8, 1024], replicated, may hold values from -20 to 20
Outputs:
- patch_out: bfloat16 [128, 128, 1024], P('row', 'col')
- register_out: bfloat16 [8, 1024], replicated
All inputs are finite; a program needn't handle non-finite values.
Results may differ from a plain program's by a relative error of at most 0.004.
Values may be sent and summed in bfloat16 or wider, within the bound.
No kernel may reach another device: no remote copies, remote signals or barrier semaphores. Data moves between devices by JAX's collectives and lax.ppermute only.
A program may use at most 64 MiB of HBM per device.

v0:
```python
import functools

import jax
import jax.numpy as jnp
import numpy as np
from jax import lax
from jax.experimental import pallas as pl
from jax.experimental.pallas import tpu as pltpu
from jax.sharding import PartitionSpec as P


HEADS = 16
PARTS = 1
TOGETHER_C = 2
TOGETHER_E = 2
RADIUS = 8
FAR = -30000.0
LEAST, MOST = 1e-20, 1e30
LANES = 128
F32 = jnp.float32
BF16 = jnp.bfloat16
NT = (((1,), (1,)), ((), ()))
NN = (((1,), (0,)), ((), ()))
TN = (((0,), (0,)), ((), ()))
VMEM = pl.BlockSpec(memory_space=pltpu.VMEM)
HBM = pl.BlockSpec(memory_space=pltpu.HBM)
SMEM = pl.BlockSpec(memory_space=pltpu.SMEM)
PARAMS = pltpu.CompilerParams(vmem_limit_bytes=24 * 1024 * 1024)


def dot(a, b, dims):
    return lax.dot_general(a, b, dims, preferred_element_type=F32)


def shift(x, axis, step):
    n = lax.axis_size(axis)
    return lax.ppermute(x, axis, [(i, i + step) for i in range(n) if 0 <= i + step < n])


def key_features(rows, cols, tr, tc):
    lane = np.arange(LANES)
    far_col = (lane < tc) & (np.abs(cols[..., None] - lane) > RADIUS)
    far_row = (lane >= tc) & (lane < tc + tr) & (np.abs(rows[..., None] - (lane - tc)) > RADIUS)
    return np.where(far_col | far_row, FAR, 0.0).astype(np.float32)


def query_features(rows, cols, tr, tc):
    lane = np.arange(LANES)
    hit = (lane == cols[..., None]) | (lane - tc == rows[..., None]) | (lane == tc + tr)
    return hit.astype(np.float32)


def with_grid_edge(const, off):
    lane = lax.broadcasted_iota(jnp.int32, const.shape, const.ndim - 1)
    return jnp.where((lane == off[1]) & off[0], FAR, jnp.asarray(const)).astype(BF16)


def copy_all(copies, sems):
    started = []
    for i, (src, dst) in enumerate(copies):
        c = pltpu.make_async_copy(src, dst, sems.at[i])
        c.start()
        started.append(c)
    return started


def stage_kernel(copies_of, a_ref, b_ref, a_out, b_out, sems):
    copies = copies_of(a_ref, a_out) + copies_of(b_ref, b_out)
    for c in copy_all(copies, sems):
        c.wait()


def whole(src, dst):
    return [(src.at[j], dst.at[j]) for j in range(2)]


def stage(copies_of, count, a, b, shape):
    a, b = (pltpu.with_memory_space_constraint(x, pltpu.HBM) for x in (a, b))
    return pl.pallas_call(
        functools.partial(stage_kernel, copies_of),
        in_specs=[HBM, HBM],
        out_specs=[VMEM, VMEM],
        out_shape=[pltpu.VMEM(shape, BF16)] * 2,
        scratch_shapes=[pltpu.SemaphoreType.DMA((2 * count,))],
        cost_estimate=pl.CostEstimate(flops=1_000_000, bytes_accessed=4_000_000, transcendentals=0),
        compiler_params=PARAMS,
    )(a, b)


def load_kernel(p_ref, out_ref, right_ref, left_ref, down_ref, up_ref, load_sems, send_sems):
    groups = out_ref.shape[1]
    tr = out_ref.shape[2]
    order = (0, groups - 1) + tuple(range(1, groups - 1))
    loads = {}
    for g in order:
        for j in (1, 2):
            loads[j, g] = (p_ref.at[j, :, pl.ds(g * RADIUS, RADIUS)], out_ref.at[j, g])
    for g in order:
        loads[0, g] = (p_ref.at[0, :, pl.ds(g * RADIUS, RADIUS)], out_ref.at[0, g])
    started = dict(zip(loads, copy_all(loads.values(), load_sems)))
    sends = []
    for g, ref in ((groups - 1, right_ref), (0, left_ref)):
        for j in (1, 2):
            started[j, g].wait()
            c = pltpu.make_async_copy(out_ref.at[j, g], ref.at[j - 1], send_sems.at[len(sends)])
            c.start()
            sends.append(c)
    for g in order[2:]:
        for j in (1, 2):
            started[j, g].wait()
    for ref, rows in ((down_ref, pl.ds(tr - RADIUS, RADIUS)), (up_ref, pl.ds(0, RADIUS))):
        for j in (1, 2):
            c = pltpu.make_async_copy(
                out_ref.at[j, :, rows], ref.at[j - 1], send_sems.at[len(sends)]
            )
            c.start()
            sends.append(c)
    for g in order:
        started[0, g].wait()
    for c in sends:
        c.wait()


def load(patches):
    _, tr, tc, width = patches.shape
    groups = tc // RADIUS
    side = jax.ShapeDtypeStruct((2, tr, RADIUS, width), BF16)
    rows = jax.ShapeDtypeStruct((2, groups, RADIUS, RADIUS, width), BF16)
    return pl.pallas_call(
        load_kernel,
        in_specs=[HBM],
        out_specs=[VMEM] + [HBM] * 4,
        out_shape=[pltpu.VMEM((3, groups, tr, RADIUS, width), BF16), side, side, rows, rows],
        scratch_shapes=[pltpu.SemaphoreType.DMA((3 * groups,)), pltpu.SemaphoreType.DMA((8,))],
        compiler_params=PARAMS,
        name="load",
    )(pltpu.with_memory_space_constraint(patches, pltpu.HBM))


def prep_kernel(scale, flag_ref, reg_ref, p_ref, part_ref):
    width = p_ref.shape[-1]
    count = reg_ref.shape[1]
    head = width // HEADS
    lane_head = lax.broadcasted_iota(jnp.int32, (HEADS, count, width), 2) // head
    own = lane_head == lax.broadcasted_iota(jnp.int32, (HEADS, count, width), 0)
    q = reg_ref[0].astype(F32) * scale
    q = jnp.where(own, q[None], 0.0).reshape(HEADS * count, width).astype(BF16)
    self_scores = dot(reg_ref[1], q, NT) + flag_ref[0]
    scores = dot(p_ref[1].reshape(-1, width), q, NT)
    high = jnp.maximum(
        jnp.max(scores, axis=0, keepdims=True), jnp.max(self_scores, axis=0, keepdims=True)
    )
    w = jnp.exp(scores - high)
    self_w = jnp.exp(self_scores - high)
    total = jnp.sum(w, axis=0, keepdims=True) + jnp.sum(self_w, axis=0, keepdims=True)
    wt = jnp.transpose(w).astype(BF16)
    acc = dot(wt, p_ref[2].reshape(-1, width), NN)
    acc = acc + dot(jnp.transpose(self_w).astype(BF16), reg_ref[2], NN)
    acc = jnp.sum(jnp.where(own, acc.reshape(HEADS, count, width), 0.0), axis=0)
    n = HEADS * count

    def spread(row):
        col = jnp.transpose(jnp.broadcast_to(row, (LANES, n))).reshape(HEADS, count, LANES)
        low = lax.broadcasted_iota(jnp.int32, (count, LANES), 1) < head
        return jnp.concatenate(
            [jnp.where(low, col[2 * p], col[2 * p + 1]) for p in range(HEADS // 2)], axis=1
        )

    part_ref[0] = acc
    part_ref[1] = spread(high)
    part_ref[2] = spread(total)


def prep(pg, registers, flag, scale):
    width = pg.shape[-1]
    count = registers.shape[1]
    return pl.pallas_call(
        functools.partial(prep_kernel, scale),
        in_specs=[SMEM, VMEM, VMEM],
        out_specs=VMEM,
        out_shape=pltpu.VMEM((3, count, width), F32),
        cost_estimate=pl.CostEstimate(
            flops=300_000_000, bytes_accessed=2_000_000, transcendentals=70_000
        ),
        compiler_params=PARAMS,
        name="prep",
    )(flag, registers, pg)


def merge(a, b):
    high = jnp.maximum(a[1], b[1])
    fa = jnp.exp(a[1] - high)
    fb = jnp.exp(b[1] - high)
    return jnp.stack([a[0] * fa + b[0] * fb, high, a[2] * fa + b[2] * fb])


def merge_all(part, late):
    for axis in ("row", "col"):
        n = lax.axis_size(axis)
        if n & (n - 1):
            every = lax.all_gather(part, axis)
            part = functools.reduce(merge, [every[i] for i in range(n)])
            continue
        step = 1
        while step < n:
            other = lax.ppermute(part, axis, [(i, i ^ step) for i in range(n)])
            if axis == "row" and 2 * step == n:
                other, late = lax.optimization_barrier((other, late))
            part = merge(part, other)
            step *= 2
    return part, late


def centre_kernel(scale, first, p_ref, up_ref, down_ref, reg_ref, qf_ref, kf_ref, in_ref, st_ref):
    _, groups, cells, width = p_ref.shape
    d = LANES
    head = width // HEADS
    edge = RADIUS * RADIUS
    low = lax.broadcasted_iota(jnp.int32, (edge, d), 1) < head
    pad = lax.broadcasted_iota(jnp.int32, (2 * RADIUS, d), 0) >= RADIUS
    off = lax.broadcasted_iota(jnp.int32, (2 * RADIUS, d), 1) == d - 1
    reg_f = jnp.where(pad & off, FAR, 0.0).astype(BF16)
    zero = jnp.zeros((RADIUS, d), BF16)

    def unit(i, half, part, exact):
        lanes = pl.ds(pl.multiple_of((i + first) * d, d), d)
        lanes_out = pl.ds(pl.multiple_of(i * d, d), d)
        rows = slice(half * edge, (half + 1) * edge)
        near = range(part, part + 3)
        span = cells + edge

        def stacked(j):
            pieces = []
            for g in near:
                own = p_ref[j, g, :, lanes]
                if half == 0:
                    pieces += [up_ref[j - 1, g, :, lanes], own]
                else:
                    pieces += [own, down_ref[j - 1, g, :, lanes]]
            return jnp.concatenate(pieces + [reg_ref[j, :, lanes], zero], axis=0)

        f = jnp.concatenate(
            [kf_ref[g, half * edge : half * edge + span] for g in near] + [reg_f], axis=0
        )
        kc = jnp.concatenate([stacked(1), f], axis=1)
        qs = []
        for g in (0, 1) if part == 0 else (groups - 1, groups - 2):
            q = p_ref[0, g, rows, lanes].astype(F32) * scale
            qf = qf_ref[g, rows]
            for x in (jnp.where(low, q, 0.0), jnp.where(low, 0.0, q)):
                qs.append(jnp.concatenate([x.astype(BF16), qf], axis=1))
        s = dot(kc, jnp.concatenate(qs, axis=0), NT)
        if exact:
            high = jnp.max(s, axis=0, keepdims=True)
            s = s - high
        else:
            high = jnp.zeros((1, s.shape[1]), F32)
        w = jnp.exp(s).astype(BF16)
        total = jnp.sum(w.astype(F32), axis=0, keepdims=True)
        yield total
        o = dot(stacked(2), w, TN)
        st_ref[i, half, part, :d] = o[:, :d]
        st_ref[i, half, part, d : d + 8] = jnp.concatenate(
            [high[:, :d], total[:, :d], jnp.zeros((6, d), F32)], axis=0
        )
        t = jnp.transpose(o[:, d:] / total[:, d:])
        t = jnp.where(low, t[:edge], t[edge:])
        in_ref[part, rows, lanes_out] = t.astype(BF16)

    run_guarded(unit, st_ref.shape[0], 4 * edge, TOGETHER_C)


def run_guarded(unit, count, lanes, together=1):
    units = [(half, part) for half in range(2) for part in range(2)]

    def both(i, exact):
        step = 1 if exact else together
        running = [
            unit(i * step + k, half, part, exact) for k in range(step) for half, part in units
        ]
        totals = [next(r) for r in running]
        for r in running:
            next(r, None)
        return totals

    def fast(i, seen):
        least, most = seen
        for total in both(i, False):
            least = jnp.where(total >= least, least, total)
            most = jnp.where(total <= most, most, total)
        return least, most

    one = jnp.ones((1, lanes), F32)
    least, most = lax.fori_loop(0, count // together, fast, (one, one))
    fine = jnp.where((least > LEAST) & (most < MOST), 1.0, 0.0)

    @pl.when(jnp.min(fine) < 0.5)
    def _():
        @pl.loop(0, count)
        def _(i):
            both(i, True)


def centre(pg, up, down, registers, qf, kf, scale, first, pairs):
    _, _, cells, _ = pg.shape
    edge = RADIUS * RADIUS
    d = LANES
    keys = 3 * (cells + edge) + 2 * RADIUS
    work = pairs * 4 * keys * 4 * edge
    return pl.pallas_call(
        functools.partial(centre_kernel, scale, first),
        in_specs=[VMEM] * 6,
        out_specs=[VMEM, VMEM],
        out_shape=[
            pltpu.VMEM((2, cells, pairs * d), BF16),
            pltpu.VMEM((pairs, 2, 2, d + 8, d), F32),
        ],
        cost_estimate=pl.CostEstimate(
            flops=work * 2 * 384, bytes_accessed=4_000_000, transcendentals=work
        ),
        compiler_params=PARAMS,
        name="centre",
    )(pg, up, down, registers, qf, kf)


def edge_kernel(
    scale, parts, p_ref, l_ref, r_ref, cu_ref, cd_ref, qf_ref, kf_ref, *refs
):
    inner, states = refs[:parts], refs[parts : 2 * parts]
    out_ref, edge_ref, sems = refs[2 * parts :]
    _, groups, cells, width = p_ref.shape
    d = LANES
    head = width // HEADS
    edge = RADIUS * RADIUS
    span = cells + edge
    low = lax.broadcasted_iota(jnp.int32, (edge, d), 1) < head
    per = states[0].shape[0]
    copies = []
    for n in range(parts):
        for part in range(2):
            g = 1 if part == 0 else groups - 2
            copies.append(
                (
                    inner[n].at[part],
                    out_ref.at[:, pl.ds(g * RADIUS, RADIUS), pl.ds(n * per * d, per * d)],
                )
            )
    started = copy_all(copies, sems)

    def unit_of(n, i, half, side, exact):
        st = states[n]
        lanes = pl.ds(pl.multiple_of((i + n * per) * d, d), d)
        cells_of = slice(half * edge, (half + 1) * edge)
        halo = l_ref if side == 0 else r_ref
        corner = cu_ref if half == 0 else cd_ref

        def keys(j):
            own = halo[j, :, lanes]
            far = corner[side, j, :, lanes]
            return jnp.concatenate([far, own] if half == 0 else [own, far], axis=0)

        f = kf_ref[side, half * edge : half * edge + span]
        kc = jnp.concatenate([keys(0), f], axis=1)
        g = 0 if side == 0 else groups - 1
        q = p_ref[0, g, cells_of, lanes].astype(F32) * scale
        qf = qf_ref[g, cells_of]
        qc = jnp.concatenate(
            [
                jnp.concatenate([x.astype(BF16), qf], axis=1)
                for x in (jnp.where(low, q, 0.0), jnp.where(low, 0.0, q))
            ],
            axis=0,
        )
        s = dot(kc, qc, NT)
        acc = st[i, half, side, :d]
        high = st[i, half, side, d : d + 1]
        total = st[i, half, side, d + 1 : d + 2]
        if exact:
            new = jnp.maximum(high, jnp.max(s, axis=0, keepdims=True))
            fade = jnp.exp(high - new)
            acc, total, high = acc * fade, total * fade, new
        w = jnp.exp(s - high).astype(BF16)
        total = total + jnp.sum(w.astype(F32), axis=0, keepdims=True)
        yield total
        acc = acc + dot(keys(1), w, TN)
        t = jnp.transpose(acc / total)
        t = jnp.where(low, t[:edge], t[edge:])
        rows_of = slice(half * RADIUS, (half + 1) * RADIUS)
        edge_ref[side, rows_of, :, lanes] = t.reshape(RADIUS, RADIUS, d).astype(BF16)

    for n in range(parts):
        run_guarded(functools.partial(unit_of, n), per, 2 * edge, TOGETHER_E)

    copies = []
    for side in range(2):
        g = 0 if side == 0 else groups - 1
        copies.append(
            (edge_ref.at[side], out_ref.at[:, pl.ds(g * RADIUS, RADIUS)])
        )
    started += copy_all(copies, sems.at[pl.ds(2 * parts, 2)])
    for c in started:
        c.wait()


def edges(pg, left, right, corner_up, corner_down, qf, kf, inner, states, scale, tr, tc):
    _, _, _, width = pg.shape
    parts = len(states)
    return pl.pallas_call(
        functools.partial(edge_kernel, scale, parts),
        in_specs=[VMEM] * (7 + 2 * parts),
        out_specs=HBM,
        out_shape=jax.ShapeDtypeStruct((tr, tc, width), BF16),
        scratch_shapes=[
            pltpu.VMEM((2, tr, RADIUS, width), BF16),
            pltpu.SemaphoreType.DMA((2 * parts + 2,)),
        ],
        cost_estimate=pl.CostEstimate(
            flops=500_000_000, bytes_accessed=3_000_000, transcendentals=800_000
        ),
        compiler_params=PARAMS,
        name="edges",
    )(pg, left, right, corner_up, corner_down, qf, kf, *inner, *states)


def local(patches, registers):
    _, tr, tc, width = patches.shape
    groups = tc // RADIUS
    cells = tr * RADIUS
    edge = RADIUS * RADIUS
    assert tr == 2 * RADIUS and groups == 4 and 2 * width == HEADS * LANES
    scale = (width // HEADS) ** (-0.5)
    row_at, row_n = lax.axis_index("row"), lax.axis_size("row")
    col_at, col_n = lax.axis_index("col"), lax.axis_size("col")

    in_vmem = lambda x: pltpu.with_memory_space_constraint(x, pltpu.VMEM)
    pg, to_right, to_left, to_down, to_up = load(patches)
    left = shift(to_right, "col", 1)
    right = shift(to_left, "col", -1)
    up = shift(to_down, "row", 1)
    down = shift(to_up, "row", -1)
    left, right = (x.reshape(2, cells, width) for x in (left, right))
    rows_shape = (2, groups, RADIUS, RADIUS, width)
    up, down = stage(whole, 2, up, down, rows_shape)
    up, down = (x.reshape(2, groups, edge, width) for x in (up, down))

    flag = jnp.where((row_at == 0) & (col_at == 0), 0.0, -1e30).astype(F32).reshape(1)
    pg = pg.reshape(3, groups, cells, width)
    part = prep(pg, registers, flag, scale)

    key_rows = np.repeat(np.arange(-RADIUS, tr + RADIUS), RADIUS)
    key_cols = np.tile(np.arange(RADIUS), tr + 2 * RADIUS)
    stack = lambda cols: np.stack([key_features(key_rows, key_cols + c, tr, tc) for c in cols])
    row = jnp.arange((tr + 2 * RADIUS) * RADIUS, dtype=jnp.int32)[None, :, None]
    off_rows = ((row < edge) & (row_at == 0)) | ((row >= edge + cells) & (row_at == row_n - 1))
    side = jnp.arange(2, dtype=jnp.int32)[:, None, None]
    off_cols = ((side == 0) & (col_at == 0)) | ((side == 1) & (col_at == col_n - 1))
    off_lane = LANES - 1
    kf = with_grid_edge(stack([g * RADIUS for g in range(groups)]), (off_rows, off_lane))
    kf_side = with_grid_edge(stack([-RADIUS, tc]), (off_rows | off_cols, off_lane))
    q_rows = np.repeat(np.arange(tr), RADIUS)
    q_cols = np.tile(np.arange(RADIUS), tr)
    qf = np.stack([query_features(q_rows, q_cols + g * RADIUS, tr, tc) for g in range(groups)])
    qf[..., off_lane] = 1.0
    qf = jnp.asarray(qf.astype(BF16))

    pairs = HEADS // 2
    parts = PARTS
    per = pairs // parts
    done = []
    for n in range(parts):
        done.append(centre(pg, up, down, registers, qf, kf, scale, n * per, per))
    near_l, near_r, first_state = lax.optimization_barrier((left, right, done[0][1]))
    done[0] = (done[0][0], first_state)
    bottom = jnp.stack([near_l[:, -edge:], near_r[:, -edge:]])
    corner_up = in_vmem(shift(bottom, "row", 1))
    top = jnp.stack([near_l[:, :edge], near_r[:, :edge]])
    corner_down = in_vmem(shift(top, "row", -1))
    part, first_state = merge_all(part, done[0][1])
    done[0] = (done[0][0], first_state)
    register_out = (part[0] / part[2]).astype(BF16)
    left, right = stage(whole, 2, near_l, near_r, left.shape)
    inner = [x[0].reshape(2, tr, RADIUS, per * LANES) for x in done]
    states = [x[1] for x in done]
    out = edges(pg, left, right, corner_up, corner_down, qf, kf_side, inner, states, scale, tr, tc)
    return (out, register_out)


def solution(mesh):
    in_specs = (P(None, "row", "col", None), P())
    out_specs = (P("row", "col", None), P())
    return jax.shard_map(local, mesh=mesh, in_specs=in_specs, out_specs=out_specs, check_vma=False)
```

profile of v0, /device:TPU:1, one launch (start us, length us, event | category | flops | bytes accessed | tf_op | source)
XLA Modules:
  0.0 74.2 jit_solution(4508076756174978233)
XLA Ops:
  0.6 3.0 %load.1 = (bf16[3,4,16,8,1024]{4,3,2,1,0:T(8,128)(2,1)S(1)}, bf16[2,16,8,1024]{3,2,1,0:T(8,128)(2,1)}, bf16[2,16,8,1024]{3,2,1,0:T(8,128)(2,1)}, bf16[2,4,8,8,10...) custom-call(bf16[3,16,32,1024]{3,2,1,0:T(8,128)(2,1)} %p_ref.1), custom_call_target="tpu_custom_call" | custom-call | tf_op jit(solution)/shard_map/load/pallas_call | solution.py:129
  3.7 4.7 %collective-permute-start = (bf16[2,16,8,1024]{3,2,1,0:T(8,128)(2,1)}, bf16[2,16,8,1024]{3,2,1,0:T(8,128)(2,1)}, u32[]{:S(2)}, u32[]{:S(2)}) collective-permute-start(bf16[2,16,8,1024]{3,2,1,0:T(8,128)(2,1)} %get-tuple-element.19), channel_id=1, source_target_pairs={{0,1},{1,2},{2,3},{4,5},{5,6},{6,7},{8,9},{9,10},{10,11},{12,13},{... | collective-permute-start | bytes 1572872 | tf_op jit(solution)/shard_map/ppermute | solution.py:37
  8.4 1.3 %collective-permute-start.1 = (bf16[2,16,8,1024]{3,2,1,0:T(8,128)(2,1)}, bf16[2,16,8,1024]{3,2,1,0:T(8,128)(2,1)}, u32[]{:S(2)}, u32[]{:S(2)}) collective-permute-start(bf16[2,16,8,1024]{3,2,1,0:T(8,128)(2,1)} %get-tuple-element.20), channel_id=1, source_target_pairs={{1,0},{2,1},{3,2},{5,4},{6,5},{7,6},{9,8},{10,9},{11,10},{13,12},{... | collective-permute-start | bytes 1572872 | tf_op jit(solution)/shard_map/ppermute | solution.py:37
  9.7 4.0 %collective-permute-start.2 = (bf16[2,4,8,8,1024]{4,3,2,1,0:T(8,128)(2,1)}, bf16[2,4,8,8,1024]{4,3,2,1,0:T(8,128)(2,1)}, u32[]{:S(2)}, u32[]{:S(2)}) collective-permute-start(bf16[2,4,8,8,1024]{4,3,2,1,0:T(8,128)(2,1)} %get-tuple-element.21), channel_id=1, source_target_pairs={{0,4},{4,8},{8,12},{12,16},{16,20},{20,24},{24,28},{1,5},{5,9},{9,... | collective-permute-start | bytes 3145736 | tf_op jit(solution)/shard_map/ppermute | solution.py:37
  13.8 1.9 %collective-permute-start.3 = (bf16[2,4,8,8,1024]{4,3,2,1,0:T(8,128)(2,1)}, bf16[2,4,8,8,1024]{4,3,2,1,0:T(8,128)(2,1)}, u32[]{:S(2)}, u32[]{:S(2)}) collective-permute-start(bf16[2,4,8,8,1024]{4,3,2,1,0:T(8,128)(2,1)} %get-tuple-element.22), channel_id=1, source_target_pairs={{4,0},{8,4},{12,8},{16,12},{20,16},{24,20},{28,24},{5,1},{9,5},{13... | collective-permute-start | bytes 3145736 | tf_op jit(solution)/shard_map/ppermute | solution.py:37
  15.7 0.0 copy-start
  15.7 1.3 %prep.1 = f32[3,8,1024]{2,1,0:T(8,128)S(1)} custom-call(f32[1]{0:T(128)} %bitcast.10.flag_ref, bf16[3,8,1024]{2,1,0:T(8,128)(2,1)S(1)} %copy-done.1, bf16[3,4,128,1024]{3,2,1,0:T(8,128)(2,1)S(1)} %bitcast.213), custom_call_target="tpu_custom_call" | custom-call | flops 300000000 | bytes 2000000 | tf_op jit(solution)/shard_map/prep/pallas_call | solution.py:177
  17.0 0.1 collective-permute-start.6
  17.2 1.1 %select_convert_fusion.kf_ref = bf16[4,256,128]{2,1,0:T(8,128)(2,1)S(1)} fusion(bf16[4,256,128]{2,1,0:T(8,128)(2,1)} %constant.136, pred[128]{0:T(512)(128)(4,1)S(1)} %iota_compare_fusion, pred[256]{0:T(512)(128)(4,1)S(1)} %and_or_fusion.1), kind=kLoop, calls=%fused_computation.2 | loop fusion | flops 262144 | bytes 524672 | tf_op jit(solution)/shard_map/convert_element_type | solution.py:55
  18.3 0.2 collective-permute-done.6
  18.5 1.7 %collective-permute-start.7 = (f32[3,8,1024]{2,1,0:T(8,128)S(1)}, f32[3,8,1024]{2,1,0:T(8,128)S(1)}, u32[]{:S(2)}, u32[]{:S(2)}) collective-permute-start(f32[3,8,1024]{2,1,0:T(8,128)S(1)} %pad_maximum_fusion.2), channel_id=1, source_target_pairs={{0,8},{4,12},{8,0},{12,4},{16,24},{20,28},{24,16},{28,20},{1,9},{5... | collective-permute-start | bytes 294920 | tf_op jit(solution)/shard_map/ppermute | solution.py:206
  20.2 0.1 broadcast_or_fusion
  20.3 7.5 %collective-permute-done.7 = f32[3,8,1024]{2,1,0:T(8,128)S(1)} collective-permute-done((f32[3,8,1024]{2,1,0:T(8,128)S(1)}, f32[3,8,1024]{2,1,0:T(8,128)S(1)}, u32[]{:S(2)}, u32[]{:S(2)}) %collective-permute-start.7) | collective-permute-done | bytes 98336 | tf_op jit(solution)/shard_map/ppermute | solution.py:206
  27.9 2.4 %collective-permute-start.8 = (f32[3,8,1024]{2,1,0:T(8,128)S(1)}, f32[3,8,1024]{2,1,0:T(8,128)S(1)}, u32[]{:S(2)}, u32[]{:S(2)}) collective-permute-start(f32[3,8,1024]{2,1,0:T(8,128)S(1)} %pad_maximum_fusion.3), channel_id=1, source_target_pairs={{0,16},{4,20},{8,24},{12,28},{16,0},{20,4},{24,8},{28,12},{1,17},{... | collective-permute-start | bytes 294920 | tf_op jit(solution)/shard_map/ppermute | solution.py:206
  30.2 1.3 %collective-permute-done.3.b_ref = bf16[2,4,8,8,1024]{4,3,2,1,0:T(8,128)(2,1)} collective-permute-done((bf16[2,4,8,8,1024]{4,3,2,1,0:T(8,128)(2,1)}, bf16[2,4,8,8,1024]{4,3,2,1,0:T(8,128)(2,1)}, u32[]{:S(2)}, u32[]{:S(2)}) %collective-permute-start.3) | collective-permute-done | bytes 1048608 | tf_op jit(solution)/shard_map/ppermute | solution.py:37
  31.5 1.5 %shard_map.68 = (bf16[2,4,8,8,1024]{4,3,2,1,0:T(8,128)(2,1)S(1)}, bf16[2,4,8,8,1024]{4,3,2,1,0:T(8,128)(2,1)S(1)}) custom-call(bf16[2,4,8,8,1024]{4,3,2,1,0:T(8,128)(2,1)} %collective-permute-done.2.a_ref, bf16[2,4,8,8,1024]{4,3,2,1,0:T(8,128)(2,1)} %collective-permute-done.3.b_ref), custom_call_target="tpu_custom_call" | custom-call | flops 1000000 | bytes 4000000 | tf_op jit(solution)/shard_map/pallas_call | solution.py:79
  33.1 17.1 %centre.1 = (bf16[2,128,1024]{2,1,0:T(8,128)(2,1)S(1)}, f32[8,2,2,136,128]{4,3,2,1,0:T(8,128)S(1)}) custom-call(bf16[3,4,128,1024]{3,2,1,0:T(8,128)(2,1)S(1)} %bitcast.214, bf16[2,4,64,1024]{3,2,1,0:T(8,128)(2,1)S(1)} %bitcast.217, bf16[2,4,64,1024]{3,2,1,0:T(8,128)(2,1)S(1)} %bitcast.218, bf16[3,8,1024]{2,1,0:T(8,128)(2,1)S(1)} %copy-done.1, ...), custom_call_target="tpu_custom_call" | custom-call | flops 3724541952 | bytes 4000000 | tf_op jit(solution)/shard_map/centre/pallas_call | solution.py:310
  50.2 0.0 copy-start.2
  50.2 1.3 %slice_bitcast_fusion = (bf16[1,2,64,1024]{3,2,1,0:T(8,128)(2,1)S(1)}, bf16[1,2,64,1024]{3,2,1,0:T(8,128)(2,1)S(1)}, bf16[1,2,64,1024]{3,2,1,0:T(8,128)(2,1)S(1)}, bf16[1,2,64,1024]{3,2,1,0:T(8,128)(2,1)S(1)}) fusion(bf16[2,128,1024]{2,1,0:T(8,128)(2,1)} %bitcast.2.b_ref, bf16[2,128,1024]{2,1,0:T(8,128)(2,1)} %bitcast.1.a_ref), kind=kLoop, calls=%fused_computation.4 | loop fusion | bytes 2097152 | tf_op jit(solution)/shard_map/stack | solution.py:476
  51.5 0.1 pad_maximum_fusion
  51.6 6.1 %collective-permute-start.4 = (bf16[2,2,64,1024]{3,2,1,0:T(8,128)(2,1)S(1)}, bf16[2,2,64,1024]{3,2,1,0:T(8,128)(2,1)S(1)}, u32[]{:S(2)}, u32[]{:S(2)}) collective-permute-start(bf16[2,2,64,1024]{3,2,1,0:T(8,128)(2,1)S(1)} %pad_maximum_fusion), channel_id=1, source_target_pairs={{0,4},{4,8},{8,12},{12,16},{16,20},{20,24},{24,28},{1,5},{5,9},{9,... | collective-permute-start | bytes 1572872 | tf_op jit(solution)/shard_map/ppermute | solution.py:37
  57.8 2.4 %collective-permute-start.9 = (f32[3,8,1024]{2,1,0:T(8,128)S(1)}, f32[3,8,1024]{2,1,0:T(8,128)S(1)}, u32[]{:S(2)}, u32[]{:S(2)}) collective-permute-start(f32[3,8,1024]{2,1,0:T(8,128)S(1)} %pad_maximum_fusion.4), channel_id=1, source_target_pairs={{0,1},{1,0},{2,3},{3,2},{4,5},{5,4},{6,7},{7,6},{8,9},{9,8},{10,11... | collective-permute-start | bytes 294920 | tf_op jit(solution)/shard_map/ppermute | solution.py:206
  60.2 0.1 pad_maximum_fusion.1
  60.2 1.9 %collective-permute-start.5 = (bf16[2,2,64,1024]{3,2,1,0:T(8,128)(2,1)S(1)}, bf16[2,2,64,1024]{3,2,1,0:T(8,128)(2,1)S(1)}, u32[]{:S(2)}, u32[]{:S(2)}) collective-permute-start(bf16[2,2,64,1024]{3,2,1,0:T(8,128)(2,1)S(1)} %pad_maximum_fusion.1), channel_id=1, source_target_pairs={{4,0},{8,4},{12,8},{16,12},{20,16},{24,20},{28,24},{5,1},{9,5},{13... | collective-permute-start | bytes 1572872 | tf_op jit(solution)/shard_map/ppermute | solution.py:37
  62.2 0.0 collective-permute-done.9
  62.2 1.8 %collective-permute-start.10 = (f32[3,8,1024]{2,1,0:T(8,128)S(1)}, f32[3,8,1024]{2,1,0:T(8,128)S(1)}, u32[]{:S(2)}, u32[]{:S(2)}) collective-permute-start(f32[3,8,1024]{2,1,0:T(8,128)S(1)} %pad_maximum_fusion.5), channel_id=1, source_target_pairs={{0,2},{1,3},{2,0},{3,1},{4,6},{5,7},{6,4},{7,5},{8,10},{9,11},{10,... | collective-permute-start | bytes 294920 | tf_op jit(solution)/shard_map/ppermute | solution.py:206
  64.0 0.1 select_convert_fusion.1.kf_ref
  64.1 1.2 %shard_map.69 = (bf16[2,128,1024]{2,1,0:T(8,128)(2,1)S(1)}, bf16[2,128,1024]{2,1,0:T(8,128)(2,1)S(1)}) custom-call(bf16[2,128,1024]{2,1,0:T(8,128)(2,1)} %bitcast.1.a_ref, bf16[2,128,1024]{2,1,0:T(8,128)(2,1)} %bitcast.2.b_ref), custom_call_target="tpu_custom_call" | custom-call | flops 1000000 | bytes 4000000 | tf_op jit(solution)/shard_map/pallas_call | solution.py:79
  65.4 0.6 collective-permute-done.10
  66.0 0.7 fusion.36
  66.7 4.0 %collective-permute-done.5.cd_ref = bf16[2,2,64,1024]{3,2,1,0:T(8,128)(2,1)S(1)} collective-permute-done((bf16[2,2,64,1024]{3,2,1,0:T(8,128)(2,1)S(1)}, bf16[2,2,64,1024]{3,2,1,0:T(8,128)(2,1)S(1)}, u32[]{:S(2)}, u32[]{:S(2)}) %collective-permute-start.5) | collective-permute-done | bytes 524320 | tf_op jit(solution)/shard_map/ppermute | solution.py:37
  70.7 3.5 %edges.1 = bf16[16,32,1024]{2,1,0:T(8,128)(2,1)} custom-call(bf16[3,4,128,1024]{3,2,1,0:T(8,128)(2,1)S(1)} %bitcast.215, bf16[2,128,1024]{2,1,0:T(8,128)(2,1)S(1)} %get-tuple-element.28.l_ref, bf16[2,128,1024]{2,1,0:T(8,128)(2,1)S(1)} %get-tuple-element.29.r_ref, bf16[2,2,64,1024]{3,2,1,0:T(8,128)(2,1)S(1)} %collective-permute-done.4.cu_ref, ...), custom_call_target="tpu_custom_call" | custom-call | flops 500000000 | bytes 3000000 | tf_op jit(solution)/shard_map/edges/pallas_call | solution.py:408
  (23 shorter events, 0.2 us)
Async XLA Ops:
  0.6 15.1 %copy-start.1 = (bf16[3,8,1024]{2,1,0:T(8,128)(2,1)S(1)}, bf16[3,8,1024]{2,1,0:T(8,128)(2,1)}, u32[]{:S(2)}) copy-start(bf16[3,8,1024]{2,1,0:T(8,128)(2,1)} %reg_ref.3) | copy-start | bytes 147460
  3.7 46.5 %collective-permute-start = (bf16[2,16,8,1024]{3,2,1,0:T(8,128)(2,1)}, bf16[2,16,8,1024]{3,2,1,0:T(8,128)(2,1)}, u32[]{:S(2)}, u32[]{:S(2)}) collective-permute-start(bf16[2,16,8,1024]{3,2,1,0:T(8,128)(2,1)} %get-tuple-element.19), channel_id=1, source_target_pairs={{0,1},{1,2},{2,3},{4,5},{5,6},{6,7},{8,9},{9,10},{10,11},{12,13},{... | collective-permute-start | bytes 1572872 | tf_op jit(solution)/shard_map/ppermute | solution.py:37
  8.4 41.8 %collective-permute-start.1 = (bf16[2,16,8,1024]{3,2,1,0:T(8,128)(2,1)}, bf16[2,16,8,1024]{3,2,1,0:T(8,128)(2,1)}, u32[]{:S(2)}, u32[]{:S(2)}) collective-permute-start(bf16[2,16,8,1024]{3,2,1,0:T(8,128)(2,1)} %get-tuple-element.20), channel_id=1, source_target_pairs={{1,0},{2,1},{3,2},{5,4},{6,5},{7,6},{9,8},{10,9},{11,10},{13,12},{... | collective-permute-start | bytes 1572872 | tf_op jit(solution)/shard_map/ppermute | solution.py:37
  9.7 20.5 %collective-permute-start.2 = (bf16[2,4,8,8,1024]{4,3,2,1,0:T(8,128)(2,1)}, bf16[2,4,8,8,1024]{4,3,2,1,0:T(8,128)(2,1)}, u32[]{:S(2)}, u32[]{:S(2)}) collective-permute-start(bf16[2,4,8,8,1024]{4,3,2,1,0:T(8,128)(2,1)} %get-tuple-element.21), channel_id=1, source_target_pairs={{0,4},{4,8},{8,12},{12,16},{16,20},{20,24},{24,28},{1,5},{5,9},{9,... | collective-permute-start | bytes 3145736 | tf_op jit(solution)/shard_map/ppermute | solution.py:37
  13.8 17.8 %collective-permute-start.3 = (bf16[2,4,8,8,1024]{4,3,2,1,0:T(8,128)(2,1)}, bf16[2,4,8,8,1024]{4,3,2,1,0:T(8,128)(2,1)}, u32[]{:S(2)}, u32[]{:S(2)}) collective-permute-start(bf16[2,4,8,8,1024]{4,3,2,1,0:T(8,128)(2,1)} %get-tuple-element.22), channel_id=1, source_target_pairs={{4,0},{8,4},{12,8},{16,12},{20,16},{24,20},{28,24},{5,1},{9,5},{13... | collective-permute-start | bytes 3145736 | tf_op jit(solution)/shard_map/ppermute | solution.py:37
  15.7 17.4 %copy-start = (bf16[4,128,128]{2,1,0:T(8,128)(2,1)S(1)}, bf16[4,128,128]{2,1,0:T(8,128)(2,1)}, u32[]{:S(2)}) copy-start(bf16[4,128,128]{2,1,0:T(8,128)(2,1)} %constant.39.clone.qf_ref) | copy-start | bytes 393220
  17.0 1.4 %collective-permute-start.6 = (f32[3,8,1024]{2,1,0:T(8,128)S(1)}, f32[3,8,1024]{2,1,0:T(8,128)S(1)}, u32[]{:S(2)}, u32[]{:S(2)}) collective-permute-start(f32[3,8,1024]{2,1,0:T(8,128)S(1)} %prep.1), channel_id=1, source_target_pairs={{0,4},{4,0},{8,12},{12,8},{16,20},{20,16},{24,28},{28,24},{1,5},{5... | collective-permute-start | bytes 294920 | tf_op jit(solution)/shard_map/ppermute | solution.py:206
  18.5 9.3 %collective-permute-start.7 = (f32[3,8,1024]{2,1,0:T(8,128)S(1)}, f32[3,8,1024]{2,1,0:T(8,128)S(1)}, u32[]{:S(2)}, u32[]{:S(2)}) collective-permute-start(f32[3,8,1024]{2,1,0:T(8,128)S(1)} %pad_maximum_fusion.2), channel_id=1, source_target_pairs={{0,8},{4,12},{8,0},{12,4},{16,24},{20,28},{24,16},{28,20},{1,9},{5... | collective-permute-start | bytes 294920 | tf_op jit(solution)/shard_map/ppermute | solution.py:206
  27.9 29.8 %collective-permute-start.8 = (f32[3,8,1024]{2,1,0:T(8,128)S(1)}, f32[3,8,1024]{2,1,0:T(8,128)S(1)}, u32[]{:S(2)}, u32[]{:S(2)}) collective-permute-start(f32[3,8,1024]{2,1,0:T(8,128)S(1)} %pad_maximum_fusion.3), channel_id=1, source_target_pairs={{0,16},{4,20},{8,24},{12,28},{16,0},{20,4},{24,8},{28,12},{1,17},{... | collective-permute-start | bytes 294920 | tf_op jit(solution)/shard_map/ppermute | solution.py:206
  50.2 13.8 %copy-start.2 = (bf16[2,256,128]{2,1,0:T(8,128)(2,1)S(1)}, bf16[2,256,128]{2,1,0:T(8,128)(2,1)}, u32[]{:S(2)}) copy-start(bf16[2,256,128]{2,1,0:T(8,128)(2,1)} %constant.137) | copy-start | bytes 393220
  51.6 15.1 %collective-permute-start.4 = (bf16[2,2,64,1024]{3,2,1,0:T(8,128)(2,1)S(1)}, bf16[2,2,64,1024]{3,2,1,0:T(8,128)(2,1)S(1)}, u32[]{:S(2)}, u32[]{:S(2)}) collective-permute-start(bf16[2,2,64,1024]{3,2,1,0:T(8,128)(2,1)S(1)} %pad_maximum_fusion), channel_id=1, source_target_pairs={{0,4},{4,8},{8,12},{12,16},{16,20},{20,24},{24,28},{1,5},{5,9},{9,... | collective-permute-start | bytes 1572872 | tf_op jit(solution)/shard_map/ppermute | solution.py:37
  57.8 4.4 %collective-permute-start.9 = (f32[3,8,1024]{2,1,0:T(8,128)S(1)}, f32[3,8,1024]{2,1,0:T(8,128)S(1)}, u32[]{:S(2)}, u32[]{:S(2)}) collective-permute-start(f32[3,8,1024]{2,1,0:T(8,128)S(1)} %pad_maximum_fusion.4), channel_id=1, source_target_pairs={{0,1},{1,0},{2,3},{3,2},{4,5},{5,4},{6,7},{7,6},{8,9},{9,8},{10,11... | collective-permute-start | bytes 294920 | tf_op jit(solution)/shard_map/ppermute | solution.py:206
  60.2 10.5 %collective-permute-start.5 = (bf16[2,2,64,1024]{3,2,1,0:T(8,128)(2,1)S(1)}, bf16[2,2,64,1024]{3,2,1,0:T(8,128)(2,1)S(1)}, u32[]{:S(2)}, u32[]{:S(2)}) collective-permute-start(bf16[2,2,64,1024]{3,2,1,0:T(8,128)(2,1)S(1)} %pad_maximum_fusion.1), channel_id=1, source_target_pairs={{4,0},{8,4},{12,8},{16,12},{20,16},{24,20},{28,24},{5,1},{9,5},{13... | collective-permute-start | bytes 1572872 | tf_op jit(solution)/shard_map/ppermute | solution.py:37
  62.2 3.8 %collective-permute-start.10 = (f32[3,8,1024]{2,1,0:T(8,128)S(1)}, f32[3,8,1024]{2,1,0:T(8,128)S(1)}, u32[]{:S(2)}, u32[]{:S(2)}) collective-permute-start(f32[3,8,1024]{2,1,0:T(8,128)S(1)} %pad_maximum_fusion.5), channel_id=1, source_target_pairs={{0,2},{1,3},{2,0},{3,1},{4,6},{5,7},{6,4},{7,5},{8,10},{9,11},{10,... | collective-permute-start | bytes 294920 | tf_op jit(solution)/shard_map/ppermute | solution.py:206
where the time goes:
time: 74.6 us; the launch traced here: 74.2 us
  starting transfers between devices  28.4 us (38%)
  Pallas kernels  27.6 us (37%)
  waiting for transfers between devices  13.6 us (18%)
  other arithmetic  2.29 us (3%)
  local copies, waits for them, and re-layouts  1.31 us (2%)
  between operations  0.93 us (1%)
    ppermute x6, starting transfers between devices, shift(): lax.ppermute(x, axis, [(i, i + step) for i in range(n) if 0 <= i + step <...  20 us
    pallas_call x1, Pallas kernels, centre(): pl.pallas_call(functools.partial(centre_kernel, scale, first), in_specs=[...  17.1 us
    ppermute x5, starting transfers between devices, merge_all(): other = lax.ppermute(part, axis, [(i, i ^ step) for i in range(n)])  8.39 us
    ppermute x5, waiting for transfers between devices, merge_all(): other = lax.ppermute(part, axis, [(i, i ^ step) for i in range(n)])  8.3 us
    ppermute x6, waiting for transfers between devices, shift(): lax.ppermute(x, axis, [(i, i + step) for i in range(n) if 0 <= i + step <...  5.34 us
    pallas_call x1, Pallas kernels, edges(): pl.pallas_call(functools.partial(edge_kernel, scale, parts), in_specs=[VM...  3.45 us
    pallas_call x1, Pallas kernels, load(): pl.pallas_call(load_kernel, in_specs=[HBM], out_specs=[VMEM] + [HBM] * 4,...  3.01 us
    pallas_call x2, Pallas kernels, stage(): pl.pallas_call(functools.partial(stage_kernel, copies_of), in_specs=[HBM,...  2.77 us
  transfers between devices with their start and end apart: 11, of which 5 were waited for; matrix products, arithmetic and copies ran while one was open for 5% of the time, Pallas kernels for 29%

commit v1 on v0

--- a/solution.py
+++ b/solution.py
@@ -12,7 +12,7 @@
 HEADS = 16
 PARTS = 1
 TOGETHER_C = 2
-TOGETHER_E = 2
+TOGETHER_E = 4
 RADIUS = 8
 FAR = -30000.0
 LEAST, MOST = 1e-20, 1e30
@@ -194,20 +194,18 @@
     return jnp.stack([a[0] * fa + b[0] * fb, high, a[2] * fa + b[2] * fb])
 
 
-def merge_all(part, late):
-    for axis in ("row", "col"):
-        n = lax.axis_size(axis)
-        if n & (n - 1):
-            every = lax.all_gather(part, axis)
-            part = functools.reduce(merge, [every[i] for i in range(n)])
-            continue
-        step = 1
-        while step < n:
-            other = lax.ppermute(part, axis, [(i, i ^ step) for i in range(n)])
-            if axis == "row" and 2 * step == n:
-                other, late = lax.optimization_barrier((other, late))
-            part = merge(part, other)
-            step *= 2
+def merge_over(part, axis, late=None):
+    n = lax.axis_size(axis)
+    if n & (n - 1):
+        every = lax.all_gather(part, axis)
+        return functools.reduce(merge, [every[i] for i in range(n)]), late
+    step = 1
+    while step < n:
+        other = lax.ppermute(part, axis, [(i, i ^ step) for i in range(n)])
+        if step == 2 and late is not None:
+            other, late = lax.optimization_barrier((other, late))
+        part = merge(part, other)
+        step *= 2
     return part, late
 
 
@@ -469,14 +467,14 @@
     done = []
     for n in range(parts):
         done.append(centre(pg, up, down, registers, qf, kf, scale, n * per, per))
-    near_l, near_r, first_state = lax.optimization_barrier((left, right, done[0][1]))
+    part, first_state = merge_over(part, "row", done[0][1])
+    near_l, near_r, first_state, part = lax.optimization_barrier((left, right, first_state, part))
     done[0] = (done[0][0], first_state)
     bottom = jnp.stack([near_l[:, -edge:], near_r[:, -edge:]])
     corner_up = in_vmem(shift(bottom, "row", 1))
     top = jnp.stack([near_l[:, :edge], near_r[:, :edge]])
     corner_down = in_vmem(shift(top, "row", -1))
-    part, first_state = merge_all(part, done[0][1])
-    done[0] = (done[0][0], first_state)
+    part, _ = merge_over(part, "col")
     register_out = (part[0] / part[2]).astype(BF16)
     left, right = stage(whole, 2, near_l, near_r, left.shape)
     inner = [x[0].reshape(2, tr, RADIUS, per * LANES) for x in done]

time: 74.6 us -> 76.5 us (1.025)
  waiting for transfers between devices: 13.6 us -> 21.9 us
  starting transfers between devices: 28.4 us -> 22.7 us
    ppermute x6, waiting for transfers between devices: 5.34 us -> 16 us  [shift(): lax.ppermute(x, axis, [(i, i + step) for i in range(n) if 0 <= i + step <...]
    ppermute x6, starting transfers between devices: 20 us -> 15.9 us  [shift(): lax.ppermute(x, axis, [(i, i + step) for i in range(n) if 0 <= i + step <...]
    ppermute x5, waiting for transfers between devices: 8.3 us -> 5.97 us  [merge_over(): other = lax.ppermute(part, axis, [(i, i ^ step) for i in range(n)])]
    ppermute x5, starting transfers between devices: 8.39 us -> 6.75 us  [merge_over(): other = lax.ppermute(part, axis, [(i, i ^ step) for i in range(n)])]
  transfers between devices with their start and end apart: 11 -> 11, of which waited for: 5 -> 5; matrix products, arithmetic and copies ran while one was open for 5% -> 3% of each run, Pallas kernels for 29% -> 28%
where the time goes in v1:
time: 76.5 us; the launch traced here: 76.2 us
  Pallas kernels  27.1 us (35%)
  starting transfers between devices  22.7 us (30%)
  waiting for transfers between devices  21.9 us (29%)
  other arithmetic  2.25 us (3%)
  local copies, waits for them, and re-layouts  1.28 us (2%)
  between operations  0.95 us (1%)
    pallas_call x1, Pallas kernels, centre(): pl.pallas_call(functools.partial(centre_kernel, scale, first), in_specs=[...  17.1 us
    ppermute x6, waiting for transfers between devices, shift(): lax.ppermute(x, axis, [(i, i + step) for i in range(n) if 0 <= i + step <...  16 us
    ppermute x6, starting transfers between devices, shift(): lax.ppermute(x, axis, [(i, i + step) for i in range(n) if 0 <= i + step <...  15.9 us
    ppermute x5, starting transfers between devices, merge_over(): other = lax.ppermute(part, axis, [(i, i ^ step) for i in range(n)])  6.75 us
    ppermute x5, waiting for transfers between devices, merge_over(): other = lax.ppermute(part, axis, [(i, i ^ step) for i in range(n)])  5.97 us
    pallas_call x1, Pallas kernels, load(): pl.pallas_call(load_kernel, in_specs=[HBM], out_specs=[VMEM] + [HBM] * 4,...  3.01 us
    pallas_call x1, Pallas kernels, edges(): pl.pallas_call(functools.partial(edge_kernel, scale, parts), in_specs=[VM...  2.91 us
    pallas_call x2, Pallas kernels, stage(): pl.pallas_call(functools.partial(stage_kernel, copies_of), in_specs=[HBM,...  2.77 us
  transfers between devices with their start and end apart: 11, of which 5 were waited for; matrix products, arithmetic and copies ran while one was open for 3% of the time, Pallas kernels for 28%

profile of v1, /device:TPU:1, one launch (start us, length us, event | category | flops | bytes accessed | tf_op | source)
XLA Modules:
  0.0 76.2 jit_solution(18277472010361755916)
XLA Ops:
  0.6 3.0 %load.1 = (bf16[3,4,16,8,1024]{4,3,2,1,0:T(8,128)(2,1)S(1)}, bf16[2,16,8,1024]{3,2,1,0:T(8,128)(2,1)}, bf16[2,16,8,1024]{3,2,1,0:T(8,128)(2,1)}, bf16[2,4,8,8,10...) custom-call(bf16[3,16,32,1024]{3,2,1,0:T(8,128)(2,1)} %p_ref.1), custom_call_target="tpu_custom_call" | custom-call | tf_op jit(solution)/shard_map/load/pallas_call | solution.py:129
  3.7 4.7 %collective-permute-start = (bf16[2,16,8,1024]{3,2,1,0:T(8,128)(2,1)}, bf16[2,16,8,1024]{3,2,1,0:T(8,128)(2,1)}, u32[]{:S(2)}, u32[]{:S(2)}) collective-permute-start(bf16[2,16,8,1024]{3,2,1,0:T(8,128)(2,1)} %get-tuple-element.20), channel_id=1, source_target_pairs={{0,1},{1,2},{2,3},{4,5},{5,6},{6,7},{8,9},{9,10},{10,11},{12,13},{... | collective-permute-start | bytes 1572872 | tf_op jit(solution)/shard_map/ppermute | solution.py:37
  8.4 1.3 %collective-permute-start.1 = (bf16[2,16,8,1024]{3,2,1,0:T(8,128)(2,1)}, bf16[2,16,8,1024]{3,2,1,0:T(8,128)(2,1)}, u32[]{:S(2)}, u32[]{:S(2)}) collective-permute-start(bf16[2,16,8,1024]{3,2,1,0:T(8,128)(2,1)} %get-tuple-element.21), channel_id=1, source_target_pairs={{1,0},{2,1},{3,2},{5,4},{6,5},{7,6},{9,8},{10,9},{11,10},{13,12},{... | collective-permute-start | bytes 1572872 | tf_op jit(solution)/shard_map/ppermute | solution.py:37
  9.7 0.0 copy-start
  9.7 1.3 %prep.1 = f32[3,8,1024]{2,1,0:T(8,128)S(1)} custom-call(f32[1]{0:T(128)} %bitcast.3.flag_ref, bf16[3,8,1024]{2,1,0:T(8,128)(2,1)S(1)} %copy-done.1, bf16[3,4,128,1024]{3,2,1,0:T(8,128)(2,1)S(1)} %bitcast.96), custom_call_target="tpu_custom_call" | custom-call | flops 300000000 | bytes 2000000 | tf_op jit(solution)/shard_map/prep/pallas_call | solution.py:177
  11.1 1.0 %collective-permute-start.2 = (f32[3,8,1024]{2,1,0:T(8,128)S(1)}, f32[3,8,1024]{2,1,0:T(8,128)S(1)}, u32[]{:S(2)}, u32[]{:S(2)}) collective-permute-start(f32[3,8,1024]{2,1,0:T(8,128)S(1)} %prep.1), channel_id=1, source_target_pairs={{0,4},{4,0},{8,12},{12,8},{16,20},{20,16},{24,28},{28,24},{1,5},{5... | collective-permute-start | bytes 294920 | tf_op jit(solution)/shard_map/ppermute | solution.py:204
  12.1 3.1 %collective-permute-start.4 = (bf16[2,4,8,8,1024]{4,3,2,1,0:T(8,128)(2,1)}, bf16[2,4,8,8,1024]{4,3,2,1,0:T(8,128)(2,1)}, u32[]{:S(2)}, u32[]{:S(2)}) collective-permute-start(bf16[2,4,8,8,1024]{4,3,2,1,0:T(8,128)(2,1)} %get-tuple-element.22), channel_id=1, source_target_pairs={{0,4},{4,8},{8,12},{12,16},{16,20},{20,24},{24,28},{1,5},{5,9},{9,... | collective-permute-start | bytes 3145736 | tf_op jit(solution)/shard_map/ppermute | solution.py:37
  15.2 2.2 %collective-permute-start.5 = (bf16[2,4,8,8,1024]{4,3,2,1,0:T(8,128)(2,1)}, bf16[2,4,8,8,1024]{4,3,2,1,0:T(8,128)(2,1)}, u32[]{:S(2)}, u32[]{:S(2)}) collective-permute-start(bf16[2,4,8,8,1024]{4,3,2,1,0:T(8,128)(2,1)} %get-tuple-element.23), channel_id=1, source_target_pairs={{4,0},{8,4},{12,8},{16,12},{20,16},{24,20},{28,24},{5,1},{9,5},{13... | collective-permute-start | bytes 3145736 | tf_op jit(solution)/shard_map/ppermute | solution.py:37
  17.4 1.1 %select_convert_fusion.kf_ref = bf16[4,256,128]{2,1,0:T(8,128)(2,1)S(1)} fusion(bf16[4,256,128]{2,1,0:T(8,128)(2,1)} %constant.103, pred[128]{0:T(512)(128)(4,1)S(1)} %iota_compare_fusion, pred[256]{0:T(512)(128)(4,1)S(1)} %and_or_fusion.1), kind=kLoop, calls=%fused_computation.2 | loop fusion | flops 262144 | bytes 524672 | tf_op jit(solution)/shard_map/convert_element_type | solution.py:55
  18.5 0.0 collective-permute-done.2
  18.6 1.1 %collective-permute-start.3 = (f32[3,8,1024]{2,1,0:T(8,128)S(1)}, f32[3,8,1024]{2,1,0:T(8,128)S(1)}, u32[]{:S(2)}, u32[]{:S(2)}) collective-permute-start(f32[3,8,1024]{2,1,0:T(8,128)S(1)} %pad_maximum_fusion.2), channel_id=1, source_target_pairs={{0,8},{4,12},{8,0},{12,4},{16,24},{20,28},{24,16},{28,20},{1,9},{5... | collective-permute-start | bytes 294920 | tf_op jit(solution)/shard_map/ppermute | solution.py:204
  19.7 8.6 %collective-permute-done.4.a_ref = bf16[2,4,8,8,1024]{4,3,2,1,0:T(8,128)(2,1)} collective-permute-done((bf16[2,4,8,8,1024]{4,3,2,1,0:T(8,128)(2,1)}, bf16[2,4,8,8,1024]{4,3,2,1,0:T(8,128)(2,1)}, u32[]{:S(2)}, u32[]{:S(2)}) %collective-permute-start.4) | collective-permute-done | bytes 1048608 | tf_op jit(solution)/shard_map/ppermute | solution.py:37
  28.3 4.5 %collective-permute-done.5.b_ref = bf16[2,4,8,8,1024]{4,3,2,1,0:T(8,128)(2,1)} collective-permute-done((bf16[2,4,8,8,1024]{4,3,2,1,0:T(8,128)(2,1)}, bf16[2,4,8,8,1024]{4,3,2,1,0:T(8,128)(2,1)}, u32[]{:S(2)}, u32[]{:S(2)}) %collective-permute-start.5) | collective-permute-done | bytes 1048608 | tf_op jit(solution)/shard_map/ppermute | solution.py:37
  32.8 1.5 %shard_map.68 = (bf16[2,4,8,8,1024]{4,3,2,1,0:T(8,128)(2,1)S(1)}, bf16[2,4,8,8,1024]{4,3,2,1,0:T(8,128)(2,1)S(1)}) custom-call(bf16[2,4,8,8,1024]{4,3,2,1,0:T(8,128)(2,1)} %collective-permute-done.4.a_ref, bf16[2,4,8,8,1024]{4,3,2,1,0:T(8,128)(2,1)} %collective-permute-done.5.b_ref), custom_call_target="tpu_custom_call" | custom-call | flops 1000000 | bytes 4000000 | tf_op jit(solution)/shard_map/pallas_call | solution.py:79
  34.4 17.1 %centre.1 = (bf16[2,128,1024]{2,1,0:T(8,128)(2,1)S(1)}, f32[8,2,2,136,128]{4,3,2,1,0:T(8,128)S(1)}) custom-call(bf16[3,4,128,1024]{3,2,1,0:T(8,128)(2,1)S(1)} %bitcast.97, bf16[2,4,64,1024]{3,2,1,0:T(8,128)(2,1)S(1)} %bitcast.100, bf16[2,4,64,1024]{3,2,1,0:T(8,128)(2,1)S(1)} %bitcast.101, bf16[3,8,1024]{2,1,0:T(8,128)(2,1)S(1)} %copy-done.1, ...), custom_call_target="tpu_custom_call" | custom-call | flops 3724541952 | bytes 4000000 | tf_op jit(solution)/shard_map/centre/pallas_call | solution.py:308
  51.5 0.0 copy-start.2
  51.6 0.1 collective-permute-start.6
  51.6 0.1 broadcast_or_fusion
  51.7 5.3 %collective-permute-done.6 = f32[3,8,1024]{2,1,0:T(8,128)S(1)} collective-permute-done((f32[3,8,1024]{2,1,0:T(8,128)S(1)}, f32[3,8,1024]{2,1,0:T(8,128)S(1)}, u32[]{:S(2)}, u32[]{:S(2)}) %collective-permute-start.6) | collective-permute-done | bytes 98336 | tf_op jit(solution)/shard_map/ppermute | solution.py:204
  57.1 1.3 %slice_bitcast_fusion = (bf16[1,2,64,1024]{3,2,1,0:T(8,128)(2,1)S(1)}, bf16[1,2,64,1024]{3,2,1,0:T(8,128)(2,1)S(1)}, bf16[1,2,64,1024]{3,2,1,0:T(8,128)(2,1)S(1)}, bf16[1,2,64,1024]{3,2,1,0:T(8,128)(2,1)S(1)}) fusion(bf16[2,128,1024]{2,1,0:T(8,128)(2,1)} %bitcast.2.b_ref, bf16[2,128,1024]{2,1,0:T(8,128)(2,1)} %bitcast.1.a_ref), kind=kLoop, calls=%fused_computation.4 | loop fusion | bytes 2097152 | tf_op jit(solution)/shard_map/stack | solution.py:475
  58.4 0.1 pad_maximum_fusion
  58.4 1.9 %collective-permute-start.7 = (bf16[2,2,64,1024]{3,2,1,0:T(8,128)(2,1)S(1)}, bf16[2,2,64,1024]{3,2,1,0:T(8,128)(2,1)S(1)}, u32[]{:S(2)}, u32[]{:S(2)}) collective-permute-start(bf16[2,2,64,1024]{3,2,1,0:T(8,128)(2,1)S(1)} %pad_maximum_fusion), channel_id=1, source_target_pairs={{0,4},{4,8},{8,12},{12,16},{16,20},{20,24},{24,28},{1,5},{5,9},{9,... | collective-permute-start | bytes 1572872 | tf_op jit(solution)/shard_map/ppermute | solution.py:37
  60.4 2.3 %collective-permute-start.9 = (f32[3,8,1024]{2,1,0:T(8,128)S(1)}, f32[3,8,1024]{2,1,0:T(8,128)S(1)}, u32[]{:S(2)}, u32[]{:S(2)}) collective-permute-start(f32[3,8,1024]{2,1,0:T(8,128)S(1)} %pad_maximum_fusion.4), channel_id=1, source_target_pairs={{0,1},{1,0},{2,3},{3,2},{4,5},{5,4},{6,7},{7,6},{8,9},{9,8},{10,11... | collective-permute-start | bytes 294920 | tf_op jit(solution)/shard_map/ppermute | solution.py:204
  62.7 0.1 pad_maximum_fusion.1
  62.7 2.7 %collective-permute-start.8 = (bf16[2,2,64,1024]{3,2,1,0:T(8,128)(2,1)S(1)}, bf16[2,2,64,1024]{3,2,1,0:T(8,128)(2,1)S(1)}, u32[]{:S(2)}, u32[]{:S(2)}) collective-permute-start(bf16[2,2,64,1024]{3,2,1,0:T(8,128)(2,1)S(1)} %pad_maximum_fusion.1), channel_id=1, source_target_pairs={{4,0},{8,4},{12,8},{16,12},{20,16},{24,20},{28,24},{5,1},{9,5},{13... | collective-permute-start | bytes 1572872 | tf_op jit(solution)/shard_map/ppermute | solution.py:37
  65.5 2.2 %collective-permute-start.10 = (f32[3,8,1024]{2,1,0:T(8,128)S(1)}, f32[3,8,1024]{2,1,0:T(8,128)S(1)}, u32[]{:S(2)}, u32[]{:S(2)}) collective-permute-start(f32[3,8,1024]{2,1,0:T(8,128)S(1)} %pad_maximum_fusion.5), channel_id=1, source_target_pairs={{0,2},{1,3},{2,0},{3,1},{4,6},{5,7},{6,4},{7,5},{8,10},{9,11},{10,... | collective-permute-start | bytes 294920 | tf_op jit(solution)/shard_map/ppermute | solution.py:204
  67.8 0.1 select_convert_fusion.1.kf_ref
  67.9 1.2 %shard_map.69 = (bf16[2,128,1024]{2,1,0:T(8,128)(2,1)S(1)}, bf16[2,128,1024]{2,1,0:T(8,128)(2,1)S(1)}) custom-call(bf16[2,128,1024]{2,1,0:T(8,128)(2,1)} %bitcast.1.a_ref, bf16[2,128,1024]{2,1,0:T(8,128)(2,1)} %bitcast.2.b_ref), custom_call_target="tpu_custom_call" | custom-call | flops 1000000 | bytes 4000000 | tf_op jit(solution)/shard_map/pallas_call | solution.py:79
  69.1 0.6 collective-permute-done.10
  69.8 0.6 fusion.19
  70.4 2.8 %collective-permute-done.8.cd_ref = bf16[2,2,64,1024]{3,2,1,0:T(8,128)(2,1)S(1)} collective-permute-done((bf16[2,2,64,1024]{3,2,1,0:T(8,128)(2,1)S(1)}, bf16[2,2,64,1024]{3,2,1,0:T(8,128)(2,1)S(1)}, u32[]{:S(2)}, u32[]{:S(2)}) %collective-permute-start.8) | collective-permute-done | bytes 524320 | tf_op jit(solution)/shard_map/ppermute | solution.py:37
  73.2 2.9 %edges.1 = bf16[16,32,1024]{2,1,0:T(8,128)(2,1)} custom-call(bf16[3,4,128,1024]{3,2,1,0:T(8,128)(2,1)S(1)} %bitcast.98, bf16[2,128,1024]{2,1,0:T(8,128)(2,1)S(1)} %get-tuple-element.31.l_ref, bf16[2,128,1024]{2,1,0:T(8,128)(2,1)S(1)} %get-tuple-element.32.r_ref, bf16[2,2,64,1024]{3,2,1,0:T(8,128)(2,1)S(1)} %collective-permute-done.7.cu_ref, ...), custom_call_target="tpu_custom_call" | custom-call | flops 500000000 | bytes 3000000 | tf_op jit(solution)/shard_map/edges/pallas_call | solution.py:406
  (23 shorter events, 0.2 us)
Async XLA Ops:
  0.6 9.1 %copy-start.1 = (bf16[3,8,1024]{2,1,0:T(8,128)(2,1)S(1)}, bf16[3,8,1024]{2,1,0:T(8,128)(2,1)}, u32[]{:S(2)}) copy-start(bf16[3,8,1024]{2,1,0:T(8,128)(2,1)} %reg_ref.3) | copy-start | bytes 147460
  3.7 53.4 %collective-permute-start = (bf16[2,16,8,1024]{3,2,1,0:T(8,128)(2,1)}, bf16[2,16,8,1024]{3,2,1,0:T(8,128)(2,1)}, u32[]{:S(2)}, u32[]{:S(2)}) collective-permute-start(bf16[2,16,8,1024]{3,2,1,0:T(8,128)(2,1)} %get-tuple-element.20), channel_id=1, source_target_pairs={{0,1},{1,2},{2,3},{4,5},{5,6},{6,7},{8,9},{9,10},{10,11},{12,13},{... | collective-permute-start | bytes 1572872 | tf_op jit(solution)/shard_map/ppermute | solution.py:37
  8.4 48.7 %collective-permute-start.1 = (bf16[2,16,8,1024]{3,2,1,0:T(8,128)(2,1)}, bf16[2,16,8,1024]{3,2,1,0:T(8,128)(2,1)}, u32[]{:S(2)}, u32[]{:S(2)}) collective-permute-start(bf16[2,16,8,1024]{3,2,1,0:T(8,128)(2,1)} %get-tuple-element.21), channel_id=1, source_target_pairs={{1,0},{2,1},{3,2},{5,4},{6,5},{7,6},{9,8},{10,9},{11,10},{13,12},{... | collective-permute-start | bytes 1572872 | tf_op jit(solution)/shard_map/ppermute | solution.py:37
  9.7 24.7 %copy-start = (bf16[4,128,128]{2,1,0:T(8,128)(2,1)S(1)}, bf16[4,128,128]{2,1,0:T(8,128)(2,1)}, u32[]{:S(2)}) copy-start(bf16[4,128,128]{2,1,0:T(8,128)(2,1)} %constant.39.clone.qf_ref) | copy-start | bytes 393220
  11.1 7.4 %collective-permute-start.2 = (f32[3,8,1024]{2,1,0:T(8,128)S(1)}, f32[3,8,1024]{2,1,0:T(8,128)S(1)}, u32[]{:S(2)}, u32[]{:S(2)}) collective-permute-start(f32[3,8,1024]{2,1,0:T(8,128)S(1)} %prep.1), channel_id=1, source_target_pairs={{0,4},{4,0},{8,12},{12,8},{16,20},{20,16},{24,28},{28,24},{1,5},{5... | collective-permute-start | bytes 294920 | tf_op jit(solution)/shard_map/ppermute | solution.py:204
  12.1 16.2 %collective-permute-start.4 = (bf16[2,4,8,8,1024]{4,3,2,1,0:T(8,128)(2,1)}, bf16[2,4,8,8,1024]{4,3,2,1,0:T(8,128)(2,1)}, u32[]{:S(2)}, u32[]{:S(2)}) collective-permute-start(bf16[2,4,8,8,1024]{4,3,2,1,0:T(8,128)(2,1)} %get-tuple-element.22), channel_id=1, source_target_pairs={{0,4},{4,8},{8,12},{12,16},{16,20},{20,24},{24,28},{1,5},{5,9},{9,... | collective-permute-start | bytes 3145736 | tf_op jit(solution)/shard_map/ppermute | solution.py:37
  15.2 17.6 %collective-permute-start.5 = (bf16[2,4,8,8,1024]{4,3,2,1,0:T(8,128)(2,1)}, bf16[2,4,8,8,1024]{4,3,2,1,0:T(8,128)(2,1)}, u32[]{:S(2)}, u32[]{:S(2)}) collective-permute-start(bf16[2,4,8,8,1024]{4,3,2,1,0:T(8,128)(2,1)} %get-tuple-element.23), channel_id=1, source_target_pairs={{4,0},{8,4},{12,8},{16,12},{20,16},{24,20},{28,24},{5,1},{9,5},{13... | collective-permute-start | bytes 3145736 | tf_op jit(solution)/shard_map/ppermute | solution.py:37
  18.6 32.9 %collective-permute-start.3 = (f32[3,8,1024]{2,1,0:T(8,128)S(1)}, f32[3,8,1024]{2,1,0:T(8,128)S(1)}, u32[]{:S(2)}, u32[]{:S(2)}) collective-permute-start(f32[3,8,1024]{2,1,0:T(8,128)S(1)} %pad_maximum_fusion.2), channel_id=1, source_target_pairs={{0,8},{4,12},{8,0},{12,4},{16,24},{20,28},{24,16},{28,20},{1,9},{5... | collective-permute-start | bytes 294920 | tf_op jit(solution)/shard_map/ppermute | solution.py:204
  51.5 16.3 %copy-start.2 = (bf16[2,256,128]{2,1,0:T(8,128)(2,1)S(1)}, bf16[2,256,128]{2,1,0:T(8,128)(2,1)}, u32[]{:S(2)}) copy-start(bf16[2,256,128]{2,1,0:T(8,128)(2,1)} %constant.104) | copy-start | bytes 393220
  51.6 5.5 %collective-permute-start.6 = (f32[3,8,1024]{2,1,0:T(8,128)S(1)}, f32[3,8,1024]{2,1,0:T(8,128)S(1)}, u32[]{:S(2)}, u32[]{:S(2)}) collective-permute-start(f32[3,8,1024]{2,1,0:T(8,128)S(1)} %pad_maximum_fusion.3), channel_id=1, source_target_pairs={{0,16},{4,20},{8,24},{12,28},{16,0},{20,4},{24,8},{28,12},{1,17},{... | collective-permute-start | bytes 294920 | tf_op jit(solution)/shard_map/ppermute | solution.py:204
  58.4 12.0 %collective-permute-start.7 = (bf16[2,2,64,1024]{3,2,1,0:T(8,128)(2,1)S(1)}, bf16[2,2,64,1024]{3,2,1,0:T(8,128)(2,1)S(1)}, u32[]{:S(2)}, u32[]{:S(2)}) collective-permute-start(bf16[2,2,64,1024]{3,2,1,0:T(8,128)(2,1)S(1)} %pad_maximum_fusion), channel_id=1, source_target_pairs={{0,4},{4,8},{8,12},{12,16},{16,20},{20,24},{24,28},{1,5},{5,9},{9,... | collective-permute-start | bytes 1572872 | tf_op jit(solution)/shard_map/ppermute | solution.py:37
  60.4 5.1 %collective-permute-start.9 = (f32[3,8,1024]{2,1,0:T(8,128)S(1)}, f32[3,8,1024]{2,1,0:T(8,128)S(1)}, u32[]{:S(2)}, u32[]{:S(2)}) collective-permute-start(f32[3,8,1024]{2,1,0:T(8,128)S(1)} %pad_maximum_fusion.4), channel_id=1, source_target_pairs={{0,1},{1,0},{2,3},{3,2},{4,5},{5,4},{6,7},{7,6},{8,9},{9,8},{10,11... | collective-permute-start | bytes 294920 | tf_op jit(solution)/shard_map/ppermute | solution.py:204
  62.7 10.5 %collective-permute-start.8 = (bf16[2,2,64,1024]{3,2,1,0:T(8,128)(2,1)S(1)}, bf16[2,2,64,1024]{3,2,1,0:T(8,128)(2,1)S(1)}, u32[]{:S(2)}, u32[]{:S(2)}) collective-permute-start(bf16[2,2,64,1024]{3,2,1,0:T(8,128)(2,1)S(1)} %pad_maximum_fusion.1), channel_id=1, source_target_pairs={{4,0},{8,4},{12,8},{16,12},{20,16},{24,20},{28,24},{5,1},{9,5},{13... | collective-permute-start | bytes 1572872 | tf_op jit(solution)/shard_map/ppermute | solution.py:37
  65.5 4.2 %collective-permute-start.10 = (f32[3,8,1024]{2,1,0:T(8,128)S(1)}, f32[3,8,1024]{2,1,0:T(8,128)S(1)}, u32[]{:S(2)}, u32[]{:S(2)}) collective-permute-start(f32[3,8,1024]{2,1,0:T(8,128)S(1)} %pad_maximum_fusion.5), channel_id=1, source_target_pairs={{0,2},{1,3},{2,0},{3,1},{4,6},{5,7},{6,4},{7,5},{8,10},{9,11},{10,... | collective-permute-start | bytes 294920 | tf_op jit(solution)/shard_map/ppermute | solution.py:204
